TPU v7x, 32 devices: a whole 2x2x4 slice. The times are simulated.
32 devices in a mesh: bucket: 4 (over y, x), seq: 8 (over z, core).
Axes of the slice: x: 2, y: 2, z: 4, core: 2. Of those that a mesh axis runs over, the one named last changes fastest.
Arguments:
- queries: bfloat16 [4, 448, 1536], P('bucket', 'seq'), may hold values from -45 to 45, as said below
- keys: bfloat16 [4, 448, 1536], P('bucket', 'seq'), may hold values from -5 to 5
- values: bfloat16 [4, 448, 1536], P('bucket', 'seq'), may hold values from -6 to 6
- bucket_lens: int32 [4], P('bucket'), may hold values from 224 to 392
- gate: float32 [4, 3072], P('bucket'), may hold values from 0.5 to 2
- out_weight: bfloat16 [1536, 3072], P(None, 'bucket'), may hold values from -0.15625 to 0.15625
Outputs:
- gated_out: bfloat16 [4, 448, 3072], P('bucket', 'seq')
Inputs may be any that keep to these rules, and one draw needn't show every extreme that they name: queries of a few tokens in a bucket may be strong multiples of some keys.
All inputs are finite; a program needn't handle non-finite values.
Results may differ from a plain program's by a relative error of at most 0.013.
Values may be sent and summed in bfloat16 or wider, within the bound.
A program may use at most 192 MiB of HBM per device.

v0:
```python
import jax
import jax.numpy as jnp
from jax import lax
from jax.sharding import PartitionSpec as P

HEADS = 12
HEAD_DIM = 128


NEG_FILL = -1e30


def block_stats(queries, keys, values, usable):
    scores = jnp.einsum(
        "qhe,nkhe->nhqk", queries, keys, preferred_element_type=jnp.float32
    ) * HEAD_DIM ** (-0.5)
    keep_mask = usable[:, None, None, :]
    scores = jnp.where(keep_mask, scores, NEG_FILL)
    maxima = jnp.max(scores, axis=3)
    weights = jnp.where(keep_mask, jnp.exp(scores - maxima[..., None]), 0.0)
    totals = jnp.sum(weights, axis=3)
    weighted = jnp.einsum(
        "nhqk,nkhe->nqhe", weights.astype(jnp.bfloat16), values, preferred_element_type=jnp.float32
    )
    divisor = jnp.transpose(jnp.maximum(totals, 1.0), (0, 2, 1))
    partial_value = (weighted / divisor[..., None]).astype(jnp.bfloat16)
    return (partial_value, jnp.transpose(maxima, (0, 2, 1)), jnp.transpose(totals, (0, 2, 1)))


def combine(partial_value, maxima, totals):
    row_max = jnp.max(maxima, axis=0)
    factors = totals * jnp.exp(maxima - row_max[None])
    summed = jnp.einsum("nqh,nqhe->qhe", factors, partial_value.astype(jnp.float32))
    attended = summed / jnp.sum(factors, axis=0)[..., None]
    return attended.reshape(attended.shape[0], -1).astype(jnp.bfloat16)


def shards(queries, keys, values, bucket_lens, gate, out_weight):
    rows_here = queries.shape[1]
    width = queries.shape[2]
    length = bucket_lens[0]
    position = lax.axis_index("seq") * rows_here + lax.iota(jnp.int32, rows_here)
    queries_all = lax.all_gather(queries[0], "seq", axis=0, tiled=True)
    count_all = queries_all.shape[0]
    key_usable = (position < length)[None, :]
    partial_value, maxima, totals = block_stats(
        queries_all.reshape(count_all, HEADS, HEAD_DIM),
        keys[0].reshape(1, rows_here, HEADS, HEAD_DIM),
        values[0].reshape(1, rows_here, HEADS, HEAD_DIM),
        key_usable,
    )
    block_max, block_total = (
        lax.all_to_all(maxima, "seq", split_axis=1, concat_axis=0, tiled=True),
        lax.all_to_all(totals, "seq", split_axis=1, concat_axis=0, tiled=True),
    )
    block_part = lax.all_to_all(
        partial_value.reshape(1, count_all, width), "seq", split_axis=1, concat_axis=0, tiled=True
    )
    shaped = block_part.reshape(block_part.shape[0], block_part.shape[1], HEADS, HEAD_DIM)
    attended = combine(shaped, block_max, block_total)
    gate_row = gate[0]
    projected = (
        jnp.dot(
            attended,
            lax.all_gather(out_weight, "bucket", axis=1, tiled=True),
            preferred_element_type=jnp.float32,
        )
        * gate_row[None, :]
    )
    result = jnp.where((position < length)[:, None], projected, 0.0).astype(jnp.bfloat16)
    return result[None]


def solution(mesh):
    placed = (
        P("bucket", "seq", None),
        P("bucket", "seq", None),
        P("bucket", "seq", None),
        P("bucket"),
        P("bucket", None),
        P(None, "bucket"),
    )
    return jax.shard_map(
        shards, mesh=mesh, in_specs=placed, out_specs=P("bucket", "seq", None), check_vma=False
    )
```

profile of v0, /device:TPU:0, one launch (start us, length us, event | category | flops | bytes accessed | tf_op | source)
XLA Modules:
  0.0 148.8 jit_solution(12838060443762022646)
XLA Ops:
  6.5 0.0 all-gather.6.cloned.1.call-start
  6.5 0.7 all-gather.6.cloned.1.call-update
  7.3 0.0 copy-start.1
  7.3 0.0 all-gather.4.cloned.1.call-start
  7.3 0.7 all-gather.4.cloned.1.call-update
  8.7 0.1 reshape.70
  8.8 0.1 reshape.73
  9.0 26.6 %all-gather.6.cloned.1.call-done = bf16[1,448,1536]{2,1,0:T(8,128)(2,1)} async-done(((bf16[1,56,1536]{2,1,0:T(8,128)(2,1)}), bf16[1,448,1536]{2,1,0:T(8,128)(2,1)}) %all-gather.6.cloned.1.call-update) | async-done | bytes 1376272 | tf_op jit(solution)/shard_map/all_gather | solution.py:43
  35.6 1.7 %copy.26 = bf16[1,448,1536]{1,2,0:T(8,128)(2,1)S(1)} copy(bf16[1,448,1536]{2,1,0:T(8,128)(2,1)} %all-gather.6.cloned.1.call-done) | data formatting | bytes 2752512 | tf_op jit(solution)/shard_map/all_gather | solution.py:43
  37.3 0.4 bitcast_reduce_fusion
  37.7 0.3 fusion.11
  38.0 0.1 copy.29
  38.2 0.6 broadcast.44
  38.8 1.2 reduce.4
  40.0 0.8 reshape.81
  40.7 3.4 %all-to-all-start = ((f32[8,1,672]{2,1,0:T(1,128)}), f32[8,1,672]{2,1,0:T(1,128)S(1)}, u32[]{:S(2)}, u32[]{:S(2)}) async-start(f32[8,1,672]{2,1,0:T(1,128)} %reshape.81), calls=%async_computation | async-start | bytes 49152 | tf_op jit(solution)/shard_map/all_to_all | solution.py:54
  44.1 0.1 copy.31
  44.3 1.2 reduce.6
  45.5 0.8 reshape.83
  46.2 3.6 %all-to-all-done = f32[8,1,672]{2,1,0:T(1,128)S(1)} async-done(((f32[8,1,672]{2,1,0:T(1,128)}), f32[8,1,672]{2,1,0:T(1,128)S(1)}, u32[]{:S(2)}, u32[]{:S(2)}) %all-to-all-start) | async-done | bytes 21536 | tf_op jit(solution)/shard_map/all_to_all | solution.py:54
  49.8 3.5 %all-to-all-start.1 = ((f32[8,1,672]{2,1,0:T(1,128)}), f32[8,1,672]{2,1,0:T(1,128)S(1)}, u32[]{:S(2)}, u32[]{:S(2)}) async-start(f32[8,1,672]{2,1,0:T(1,128)} %reshape.83), calls=%async_computation.1 | async-start | bytes 49152 | tf_op jit(solution)/shard_map/all_to_all | solution.py:53
  53.3 1.5 fusion.3
  54.8 1.6 %copy.34 = bf16[1,448,12,128]{1,3,2,0:T(8,128)(2,1)} copy(bf16[1,448,12,128]{3,1,2,0:T(8,128)(2,1)S(1)} %fusion.3) | data formatting | bytes 2752512 | tf_op jit(solution)/shard_map/convert_element_type | solution.py:26
  56.4 7.6 %copy.35 = bf16[1,448,1536]{2,0,1:T(2,128)(2,1)S(1)} copy(bf16[1,448,1536]{1,2,0:T(8,128)(2,1)} %bitcast.72) | data formatting | bytes 2752512 | tf_op jit(solution)/shard_map/reshape | solution.py:57
  64.0 0.5 broadcast.48
  64.5 10.1 %reduce.8 = bf16[448,1536]{1,0:T(8,128)(2,1)} reduce(bf16[448,1,1536]{2,1,0:T(2,128)(2,1)S(1)} %bitcast.71, bf16[]{:T(256)} %broadcast.48), dimensions={1}, to_apply=%bitcast.64.reduce_sub_computation | reduce | bytes 2752514
  74.6 4.6 %reshape.85 = bf16[8,2,43008]{2,1,0:T(2,128)(2,1)} reshape(bf16[448,1536]{1,0:T(8,128)(2,1)} %reduce.8) | data formatting | bytes 2752512
  79.2 0.0 all-to-all-done.1
  79.2 4.8 %all-to-all-start.2 = ((bf16[8,2,43008]{2,1,0:T(2,128)(2,1)}), bf16[8,2,43008]{2,1,0:T(2,128)(2,1)}, u32[]{:S(2)}, u32[]{:S(2)}) async-start(bf16[8,2,43008]{2,1,0:T(2,128)(2,1)} %reshape.85), calls=%async_computation.2 | async-start | bytes 2752512 | tf_op jit(solution)/shard_map/all_to_all | solution.py:56
  84.0 0.7 reduce.5
  84.7 0.4 reshape.82
  85.1 0.1 copy.41
  85.2 0.7 reduce.7
  85.9 0.4 reshape.84
  86.3 0.1 copy.42
  86.5 0.1 copy.43
  86.6 0.2 copy.38
  86.8 0.1 copy.36
  86.9 30.8 %all-to-all-done.2 = bf16[8,2,43008]{2,1,0:T(2,128)(2,1)} async-done(((bf16[8,2,43008]{2,1,0:T(2,128)(2,1)}), bf16[8,2,43008]{2,1,0:T(2,128)(2,1)}, u32[]{:S(2)}, u32[]{:S(2)}) %all-to-all-start.2) | async-done | bytes 1376288 | tf_op jit(solution)/shard_map/all_to_all | solution.py:56
  117.7 4.5 %reshape.86 = bf16[448,1,1536]{2,1,0:T(2,128)(2,1)S(1)} reshape(bf16[8,2,43008]{2,1,0:T(2,128)(2,1)} %all-to-all-done.2) | data formatting | bytes 2752512
  122.2 9.2 %bitcast_reduce_fusion.1 = bf16[448,1536]{1,0:T(8,128)(2,1)} fusion(bf16[448,1,1536]{2,1,0:T(2,128)(2,1)S(1)} %reshape.86), kind=kLoop, calls=%fused_computation.34 | loop fusion | bytes 2752512 | tf_op jit(solution)/shard_map/all_to_all | solution.py:56
  131.5 3.0 %reshape.75 = bf16[8,56,12,128]{3,2,1,0:T(8,128)(2,1)S(1)} reshape(bf16[448,1536]{1,0:T(8,128)(2,1)} %bitcast_reduce_fusion.1) | data formatting | bytes 2752512 | tf_op jit(solution)/shard_map/reshape | solution.py:59
  134.5 0.0 copy-start.2
  134.5 1.2 fusion.7
  135.6 0.2 fusion.17
  135.9 0.0 all-gather.4.cloned.1.call-done
  135.9 0.0 copy-done.2
  135.9 6.1 %fusion.2 = bf16[1,56,3072]{2,1,0:T(8,128)(2,1)} fusion(bf16[1536,3072]{1,0:T(8,128)(2,1)} %all-gather.4.cloned.1.call-done, f32[3072]{0:T(1024)S(1)} %bitcast.82, pred[56]{0:T(512)(128)(4,1)S(1)} %add_compare_fusion, bf16[7,8,12,128]{3,2,1,0:T(8,128)(2,1)S(1)} %bitcast.76), kind=kOutput, calls=%fused_computation.3 | convolution fusion | flops 528998400 | bytes 9965624 | tf_op jit(solution)/shard_map/dot_general | solution.py:63
  (8 shorter events, 0.1 us)
Async XLA Ops:
  6.5 2.1 %copy-start = (bf16[1,56,1536]{2,1,0:T(8,128)(2,1)S(1)}, bf16[1,56,1536]{2,1,0:T(8,128)(2,1)}, u32[]{:S(2)}) copy-start(bf16[1,56,1536]{2,1,0:T(8,128)(2,1)} %param.7) | copy-start | bytes 516100
  6.5 29.0 %all-gather.6.cloned.1.call-start = ((), (), s32[]{:S(2)}) async-start(), calls=%async_computation.4 | async-start | bytes 1548288 | tf_op jit(solution)/shard_map/all_gather | solution.py:43
  7.3 1.6 %copy-start.1 = (bf16[1,56,1536]{2,1,0:T(8,128)(2,1)S(1)}, bf16[1,56,1536]{2,1,0:T(8,128)(2,1)}, u32[]{:S(2)}) copy-start(bf16[1,56,1536]{2,1,0:T(8,128)(2,1)} %param.8) | copy-start | bytes 516100
  7.3 128.6 %all-gather.4.cloned.1.call-start = ((), (), s32[]{:S(2)}) async-start(), calls=%async_computation.3 | async-start | bytes 11796480 | tf_op jit(solution)/shard_map/all_gather | solution.py:65
  40.7 9.0 %all-to-all-start = ((f32[8,1,672]{2,1,0:T(1,128)}), f32[8,1,672]{2,1,0:T(1,128)S(1)}, u32[]{:S(2)}, u32[]{:S(2)}) async-start(f32[8,1,672]{2,1,0:T(1,128)} %reshape.81), calls=%async_computation | async-start | bytes 49152 | tf_op jit(solution)/shard_map/all_to_all | solution.py:54
  49.8 29.4 %all-to-all-start.1 = ((f32[8,1,672]{2,1,0:T(1,128)}), f32[8,1,672]{2,1,0:T(1,128)S(1)}, u32[]{:S(2)}, u32[]{:S(2)}) async-start(f32[8,1,672]{2,1,0:T(1,128)} %reshape.83), calls=%async_computation.1 | async-start | bytes 49152 | tf_op jit(solution)/shard_map/all_to_all | solution.py:53
  79.2 38.5 %all-to-all-start.2 = ((bf16[8,2,43008]{2,1,0:T(2,128)(2,1)}), bf16[8,2,43008]{2,1,0:T(2,128)(2,1)}, u32[]{:S(2)}, u32[]{:S(2)}) async-start(bf16[8,2,43008]{2,1,0:T(2,128)(2,1)} %reshape.85), calls=%async_computation.2 | async-start | bytes 2752512 | tf_op jit(solution)/shard_map/all_to_all | solution.py:56
  134.5 1.4 copy-start.2
Sparse Core Ops, SparseCore 0:
  9.0 26.5 all-gather.5
  37.4 95.8 all-gather.3
where the time goes:
time: 150 us; the launch traced here: 149 us
  waiting for transfers between devices  62.4 us (42%)
  local copies, waits for them, and re-layouts  36.7 us (24%)
  other arithmetic  14.5 us (10%)
  between operations  14.3 us (10%)
  starting transfers between devices  11.7 us (8%)
  matrix products  9.18 us (6%)
    all_to_all x1, waiting for transfers between devices, shards(): lax.all_to_all(partial_value.reshape(1, count_all, width), 'seq', split_a...  30.8 us
    all_gather x1, waiting for transfers between devices, shards(): queries_all = lax.all_gather(queries[0], 'seq', axis=0, tiled=True)  26.6 us
    unnamed x15, local copies, waits for them, and re-layouts  12.6 us
    unnamed x3, other arithmetic  12.5 us
    all_to_all x1, local copies, waits for them, and re-layouts, shards(): lax.all_to_all(partial_value.reshape(1, count_all, width), 'seq', split_a...  9.25 us
    reshape x1, local copies, waits for them, and re-layouts, shards(): partial_value.reshape(1, count_all, width)  7.59 us
    dot_general x1, matrix products, shards(): jnp.dot(attended, lax.all_gather(out_weight, 'bucket', axis=1, tiled=True...  6.12 us
    all_to_all x1, starting transfers between devices, shards(): lax.all_to_all(partial_value.reshape(1, count_all, width), 'seq', split_a...  4.82 us
  transfers between devices with their start and end apart: 5, of which 3 were waited for; matrix products, arithmetic and copies ran while one was open for 36% of the time, Pallas kernels for 0%

commit v1 on v0

--- a/solution.py
+++ b/solution.py
@@ -1,11 +1,15 @@
+import functools
+
 import jax
 import jax.numpy as jnp
 from jax import lax
+from jax.experimental import pallas as pl
+from jax.experimental.pallas import tpu as pltpu
 from jax.sharding import PartitionSpec as P
 
 HEADS = 12
 HEAD_DIM = 128
-
+CORES = 2
 
 NEG_FILL = -1e30
 
@@ -71,6 +75,225 @@
     return result[None]
 
 
+def remote(src, dst, send, recv, where):
+    return pltpu.make_async_remote_copy(
+        src_ref=src, dst_ref=dst, send_sem=send, recv_sem=recv,
+        device_id=where, device_id_type=pl.DeviceIdType.MESH,
+    )
+
+
+def stack_rows(blocks):
+    wide = jnp.concatenate([block.astype(jnp.float32) for block in blocks], axis=0)
+    return wide.astype(jnp.bfloat16)
+
+
+def fused_kernel(
+    nb, nz, len_ref, q_hbm, k_hbm, v_hbm, w_hbm, out_ref,
+    own, weight, qbuf, kvbuf, att, xbuf, ybuf,
+    load_sem, slot_sem, w_sem, a_send, a_recv, c_send, c_recv,
+    r_send, r_recv, m_send, m_recv, y_send, y_recv,
+):
+    rows = qbuf.shape[1]
+    span = qbuf.shape[2]
+    cols = weight.shape[1]
+    bucket = lax.axis_index("bucket")
+    seq = lax.axis_index("seq")
+    z = seq // CORES
+    core = lax.rem(seq, CORES)
+    steps = [1, nz - 1] + list(range(2, nz - 1)) if nz > 2 else list(range(1, nz))
+    others = [lax.rem(z + step, nz) for step in steps]
+    peers = [lax.rem(bucket + step, nb) for step in range(1, nb)]
+    partner = (bucket, z * CORES + (1 - core))
+
+    def chip(other):
+        return (bucket, other * CORES + core)
+
+    loads = []
+    for kind, ref in ((1, k_hbm), (0, q_hbm), (2, v_hbm)):
+        copy = pltpu.make_async_copy(ref.at[0], own.at[kind], load_sem.at[kind])
+        copy.start()
+        loads.append(copy)
+    columns = pl.ds(pl.multiple_of(z * span, 128), span)
+    slots = [
+        pltpu.make_async_copy(q_hbm.at[0, :, columns], qbuf.at[z], slot_sem.at[0]),
+        pltpu.make_async_copy(k_hbm.at[0, :, columns], kvbuf.at[0, seq], slot_sem.at[1]),
+        pltpu.make_async_copy(v_hbm.at[0, :, columns], kvbuf.at[1, seq], slot_sem.at[2]),
+    ]
+    for copy in slots:
+        copy.start()
+    w_copy = pltpu.make_async_copy(w_hbm, weight, w_sem)
+    w_copy.start()
+
+    barrier = pltpu.get_barrier_semaphore()
+    friends = [partner] + [chip(o) for o in others] + [(p, seq) for p in peers]
+    for friend in friends:
+        pl.semaphore_signal(
+            barrier, inc=1, device_id=friend, device_id_type=pl.DeviceIdType.MESH
+        )
+    for copy in loads + slots:
+        copy.wait()
+    pl.semaphore_wait(barrier, len(friends))
+
+    pending = []
+    for kind in (1, 0, 2):
+        for other in others:
+            part = own.at[kind, :, pl.ds(pl.multiple_of(other * span, 128), span)]
+            target = qbuf.at[z] if kind == 0 else kvbuf.at[kind - 1, seq]
+            copy = remote(
+                part, target, a_send.at[kind, other], a_recv.at[kind, z], chip(other)
+            )
+            copy.start()
+            pending.append(copy)
+
+    def arrived(kind, other):
+        place = qbuf.at[other] if kind == 0 else kvbuf.at[kind - 1, other * CORES + core]
+        remote(place, place, a_send.at[kind, other], a_recv.at[kind, other], partner).wait_recv()
+
+    def share(kind, other):
+        place = kvbuf.at[kind - 1, other * CORES + core]
+        copy = remote(
+            place, place, c_send.at[kind - 1, other], c_recv.at[kind - 1, other], partner
+        )
+        copy.start()
+        pending.append(copy)
+
+    def shared(kind):
+        for other in range(nz):
+            place = kvbuf.at[kind - 1, other * CORES + (1 - core)]
+            remote(
+                place, place, c_send.at[kind - 1, other], c_recv.at[kind - 1, other], partner
+            ).wait_recv()
+
+    share(1, z)
+    share(2, z)
+    for other in others:
+        arrived(1, other)
+        share(1, other)
+    for other in others:
+        arrived(0, other)
+    shared(1)
+    for other in others:
+        arrived(2, other)
+        share(2, other)
+
+    length = len_ref[0]
+    heads = span // HEAD_DIM
+    blocks = nz * CORES
+    query_all = stack_rows([qbuf[i] for i in range(nz)])
+    key_all = stack_rows([kvbuf[0, j] for j in range(blocks)])
+    usable = lax.broadcasted_iota(jnp.int32, (blocks * rows, nz * rows), 0) < length
+    probs = []
+    sums = []
+    for h in range(heads):
+        lanes = slice(h * HEAD_DIM, (h + 1) * HEAD_DIM)
+        scores = lax.dot_general(
+            key_all[:, lanes], query_all[:, lanes], (((1,), (1,)), ((), ())),
+            preferred_element_type=jnp.float32,
+        ) * HEAD_DIM ** (-0.5)
+        scores = jnp.where(usable, scores, NEG_FILL)
+        top = jnp.max(scores, axis=0, keepdims=True)
+        prob = jnp.exp(scores - top)
+        sums.append(jnp.sum(prob, axis=0, keepdims=True))
+        probs.append(prob.astype(jnp.bfloat16))
+    shared(2)
+    value_all = stack_rows([kvbuf[1, j] for j in range(blocks)])
+    lane = lax.broadcasted_iota(jnp.int32, (1, nz * rows), 1)
+    token = lane + (lane // rows) * ((CORES - 1) * rows) + core * rows
+    for h in range(heads):
+        lanes = slice(h * HEAD_DIM, (h + 1) * HEAD_DIM)
+        summed = lax.dot_general(
+            value_all[:, lanes], probs[h], (((0,), (0,)), ((), ())),
+            preferred_element_type=jnp.float32,
+        )
+        normal = jnp.where(token < length, summed / sums[h], 0.0).T
+        for i in range(nz):
+            att[i, :, lanes] = normal[i * rows:(i + 1) * rows].astype(jnp.bfloat16)
+
+    for other in others:
+        copy = remote(
+            att.at[other], xbuf.at[bucket, z], r_send.at[other], r_recv.at[z], chip(other)
+        )
+        copy.start()
+        pending.append(copy)
+    xbuf[bucket, z] = att[z]
+
+    def spread(source, other):
+        for peer in peers:
+            copy = remote(
+                source, xbuf.at[bucket, other],
+                m_send.at[peer, other], m_recv.at[bucket, other], (peer, seq),
+            )
+            copy.start()
+            pending.append(copy)
+
+    spread(att.at[z], z)
+    for other in others:
+        place = xbuf.at[bucket, other]
+        remote(place, place, r_send.at[other], r_recv.at[other], partner).wait_recv()
+        spread(place, other)
+
+    w_copy.wait()
+    here = pl.ds(pl.multiple_of(bucket * cols, 128), cols)
+
+    def project(which):
+        left = jnp.concatenate([xbuf[which, i] for i in range(nz)], axis=1)
+        return jnp.dot(left, weight[...], preferred_element_type=jnp.float32).astype(jnp.bfloat16)
+
+    out_ref[:, here] = project(bucket)
+    for peer in peers:
+        for other in range(nz):
+            place = xbuf.at[peer, other]
+            remote(
+                place, place, m_send.at[peer, other], m_recv.at[peer, other], partner
+            ).wait_recv()
+        ybuf[peer] = project(peer)
+        copy = remote(
+            ybuf.at[peer], out_ref.at[:, here], y_send.at[peer], y_recv.at[bucket], (peer, seq)
+        )
+        copy.start()
+        pending.append(copy)
+    for peer in peers:
+        place = out_ref.at[:, pl.ds(pl.multiple_of(peer * cols, 128), cols)]
+        remote(ybuf.at[peer], place, y_send.at[peer], y_recv.at[peer], partner).wait_recv()
+    for copy in pending:
+        copy.wait_send()
+
+
+def fused_shards(nb, nz, queries, keys, values, bucket_lens, gate, out_weight):
+    rows, width = queries.shape[1:]
+    cols = out_weight.shape[1]
+    span = width // nz
+    low = jnp.bfloat16
+    dma = pltpu.SemaphoreType.DMA
+    anywhere = pl.BlockSpec(memory_space=pl.ANY)
+    projected = pl.pallas_call(
+        functools.partial(fused_kernel, nb, nz),
+        out_shape=jax.ShapeDtypeStruct((rows, nb * cols), low),
+        in_specs=[pl.BlockSpec(memory_space=pltpu.SMEM)] + [anywhere] * 4,
+        out_specs=pl.BlockSpec(memory_space=pltpu.VMEM),
+        scratch_shapes=[
+            pltpu.VMEM((3, rows, width), low),
+            pltpu.VMEM((width, cols), low),
+            pltpu.VMEM((nz, rows, span), low),
+            pltpu.VMEM((2, nz * CORES, rows, span), low),
+            pltpu.VMEM((nz, rows, span), low),
+            pltpu.VMEM((nb, nz, rows, span), low),
+            pltpu.VMEM((nb, rows, cols), low),
+            dma((3,)), dma((3,)), dma,
+            dma((3, nz)), dma((3, nz)),
+            dma((2, nz)), dma((2, nz)),
+            dma((nz,)), dma((nz,)),
+            dma((nb, nz)), dma((nb, nz)),
+            dma((nb,)), dma((nb,)),
+        ],
+        compiler_params=pltpu.CompilerParams(collective_id=0, has_side_effects=True),
+    )(bucket_lens, queries, keys, values, out_weight)
+    position = lax.axis_index("seq") * rows + lax.iota(jnp.int32, rows)
+    gated = projected.astype(jnp.float32) * gate[0][None, :]
+    keep = (position < bucket_lens[0])[:, None]
+    return jnp.where(keep, gated, 0.0).astype(jnp.bfloat16)[None]
+
+
 def solution(mesh):
     placed = (
         P("bucket", "seq", None),
@@ -80,6 +303,10 @@
         P("bucket", None),
         P(None, "bucket"),
     )
+    nb, ns = mesh.shape["bucket"], mesh.shape["seq"]
+    body = shards
+    if ns % CORES == 0 and HEADS % (ns // CORES) == 0:
+        body = functools.partial(fused_shards, nb, ns // CORES)
     return jax.shard_map(
-        shards, mesh=mesh, in_specs=placed, out_specs=P("bucket", "seq", None), check_vma=False
-    )
+        body, mesh=mesh, in_specs=placed, out_specs=P("bucket", "seq", None), check_vma=False
+    )

time: 150 us -> 39.8 us (0.27)
  waiting for transfers between devices: 62.4 us -> 0 us
  Pallas kernels: 0 us -> 37.1 us
  local copies, waits for them, and re-layouts: 36.7 us -> 0.01 us
  between operations: 14.3 us -> 0.69 us
  other arithmetic: 14.5 us -> 1.82 us
  starting transfers between devices: 11.7 us -> 0 us
  matrix products: 9.18 us -> 0 us
    pallas_call x0 -> x1, Pallas kernels: none -> 37.1 us  [fused_shards(): pl.pallas_call(functools.partial(fused_kernel, nb, nz), out_shape=jax.Sha...]
    all_to_all x3 -> x0, waiting for transfers between devices: 34.3 us -> none  [the longest x1 30.8 us: shards(): lax.all_to_all(partial_value.reshape(1, count_all, width), 'seq', split_a...]
    all_gather x2 -> x0, waiting for transfers between devices: 26.6 us -> none  [the longest x1 26.6 us: shards(): queries_all = lax.all_gather(queries[0], 'seq', axis=0, tiled=True)]
    unnamed x15 -> x2, local copies, waits for them, and re-layouts: 12.6 us -> 0.01 us
    unnamed x3 -> x0, other arithmetic: 12.5 us -> none
    all_to_all x3 -> x0, starting transfers between devices: 11.7 us -> none  [the longest x1 4.82 us: shards(): lax.all_to_all(partial_value.reshape(1, count_all, width), 'seq', split_a...]
    reshape x2 -> x0, local copies, waits for them, and re-layouts: 10.6 us -> none  [the longest x1 7.59 us: shards(): partial_value.reshape(1, count_all, width)]
    all_to_all x3 -> x0, local copies, waits for them, and re-layouts: 9.49 us -> none  [the longest x1 9.25 us: shards(): lax.all_to_all(partial_value.reshape(1, count_all, width), 'seq', split_a...]
  transfers between devices with their start and end apart: 5 -> 0, of which waited for: 3 -> 0; matrix products, arithmetic and copies ran while one was open for 36% -> 0% of each run, Pallas kernels for 0% -> 0%
where the time goes in v1:
time: 39.8 us; the launch traced here: 39.6 us
  Pallas kernels  37.1 us (93%)
  other arithmetic  1.82 us (5%)
  between operations  0.69 us (2%)
    pallas_call x1, Pallas kernels, fused_shards(): pl.pallas_call(functools.partial(fused_kernel, nb, nz), out_shape=jax.Sha...  37.1 us
    broadcast_in_dim x1, other arithmetic, fused_shards(): return jnp.where(keep, gated, 0.0).astype(jnp.bfloat16)[None]  1.82 us

profile of v1, /device:TPU:0, one launch (start us, length us, event | category | flops | bytes accessed | tf_op | source)
XLA Modules:
  0.0 39.6 jit_solution(8559370988098460545)
XLA Ops:
  0.0 0.0 copy-start
  0.7 37.1 %shard_map.64 = bf16[56,3072]{1,0:T(8,128)(2,1)} custom-call(s32[1]{0:T(128)} %copy.7.len_ref, bf16[1,56,1536]{2,1,0:T(8,128)(2,1)} %q_hbm.1, bf16[1,56,1536]{2,1,0:T(8,128)(2,1)} %k_hbm.1, bf16[1,56,1536]{2,1,0:T(8,128)(2,1)} %v_hbm.1, bf16[1536,768]{1,0:T(8,128)(2,1)} %w_hbm.1), custom_call_target="tpu_custom_call" | custom-call | tf_op jit(solution)/shard_map/pallas_call | solution.py:269
  37.7 0.0 copy-done
  37.8 1.8 %fusion = bf16[1,56,3072]{2,1,0:T(8,128)(2,1)} fusion(bf16[56,3072]{1,0:T(8,128)(2,1)} %shard_map.64, f32[3072]{0:T(1024)S(1)} %bitcast.5, pred[56]{0:T(512)(128)(4,1)S(1)} %add_compare_fusion), kind=kLoop, calls=%fused_computation.1 | loop fusion | flops 688128 | bytes 700472 | tf_op jit(solution)/shard_map/broadcast_in_dim | solution.py:294
  (1 shorter events, 0.0 us)
Async XLA Ops:
  0.0 37.7 %copy-start = (f32[1,3072]{1,0:T(1,128)S(1)}, f32[1,3072]{1,0:T(1,128)}, u32[]{:S(2)}) copy-start(f32[1,3072]{1,0:T(1,128)} %param.10) | copy-start | bytes 36868

commit v2 on v0

--- a/solution.py
+++ b/solution.py
@@ -1,11 +1,16 @@
+import functools
+
 import jax
 import jax.numpy as jnp
 from jax import lax
+from jax.experimental import pallas as pl
+from jax.experimental.pallas import tpu as pltpu
 from jax.sharding import PartitionSpec as P
 
 HEADS = 12
 HEAD_DIM = 128
-
+CORES = 2
+CHUNKS = 2
 
 NEG_FILL = -1e30
 
@@ -71,6 +76,310 @@
     return result[None]
 
 
+def remote(src, dst, send, recv, where):
+    return pltpu.make_async_remote_copy(
+        src_ref=src, dst_ref=dst, send_sem=send, recv_sem=recv,
+        device_id=where, device_id_type=pl.DeviceIdType.MESH,
+    )
+
+
+def stack_rows(blocks):
+    wide = jnp.concatenate([block.astype(jnp.float32) for block in blocks], axis=0)
+    return wide.astype(jnp.bfloat16)
+
+
+def row_chunks(rows):
+    if CHUNKS == 1 or rows % 8 != 0 or rows < 32:
+        return [(0, rows)]
+    head = (rows // 2 + 15) // 16 * 16
+    return [(0, head), (head, rows - head)]
+
+
+def fused_kernel(nb, nz, chunks, len_ref, q_hbm, k_hbm, v_hbm, w_hbm, out_ref, *refs):
+    (
+        own, weight, kvbuf, load_sem, slot_sem, w_sem, a_send, a_recv, q_send, q_recv,
+        c_send, c_recv, r_send, r_recv, m_send, m_recv, y_send, y_recv,
+    ) = refs[:18]
+    count = len(chunks)
+    qbufs, atts, xbufs, ybufs = [refs[18 + n * count:18 + (n + 1) * count] for n in range(4)]
+    _, _, rows, span = kvbuf.shape
+    cols = weight.shape[1]
+    bucket = lax.axis_index("bucket")
+    seq = lax.axis_index("seq")
+    z = seq // CORES
+    core = lax.rem(seq, CORES)
+    last = nz * CORES - 1
+    alive = seq < last
+    steps = [1, nz - 1] + list(range(2, nz - 1)) if nz > 2 else list(range(1, nz))
+    others = [lax.rem(z + step, nz) for step in steps]
+    peers = [lax.rem(bucket + step, nb) for step in range(1, nb)]
+    if nb & (nb - 1) == 0:
+        peers = [lax.bitwise_xor(bucket, step) for step in range(1, nb)]
+    partner = (bucket, z * CORES + (1 - core))
+
+    def chip(other):
+        return (bucket, other * CORES + core)
+
+    def holds(other, which):
+        return other * CORES + which < last
+
+    barrier = pltpu.get_barrier_semaphore()
+    friends = [chip(o) for o in reversed(others)] + [(p, seq) for p in peers] + [partner]
+    for friend in friends:
+        pl.semaphore_signal(
+            barrier, inc=1, device_id=friend, device_id_type=pl.DeviceIdType.MESH
+        )
+
+    loads = []
+    for kind, ref in ((1, k_hbm), (0, q_hbm), (2, v_hbm)):
+        loads.append(pltpu.make_async_copy(ref.at[0], own.at[kind], load_sem.at[kind]))
+    mine = pl.ds(pl.multiple_of(z * span, 128), span)
+    for kind, ref in ((0, k_hbm), (1, v_hbm)):
+        loads.append(
+            pltpu.make_async_copy(ref.at[0, :, mine], kvbuf.at[kind, seq], slot_sem.at[kind])
+        )
+    for copy in loads:
+        copy.start()
+    w_copy = pltpu.make_async_copy(w_hbm, weight, w_sem)
+    w_copy.start()
+    for copy in loads:
+        copy.wait()
+    pl.semaphore_wait(barrier, len(friends))
+
+    def lanes_of(other):
+        return pl.ds(pl.multiple_of(other * span, 128), span)
+
+    def send_keys(kind, other):
+        return remote(
+            own.at[1 + kind, :, lanes_of(other)], kvbuf.at[kind, seq],
+            a_send.at[kind, other], a_recv.at[kind, z], chip(other),
+        )
+
+    def send_queries(c, other):
+        start, size = chunks[c]
+        return remote(
+            own.at[0, pl.ds(start, size), lanes_of(other)], qbufs[c].at[z],
+            q_send.at[c, other], q_recv.at[c, z], chip(other),
+        )
+
+    def share(kind, other, which):
+        place = kvbuf.at[kind, other * CORES + which]
+        return remote(
+            place, place, c_send.at[kind, other], c_recv.at[kind, other], partner
+        )
+
+    def back(c, other):
+        return remote(
+            atts[c].at[other], xbufs[c].at[bucket, z], r_send.at[c, other], r_recv.at[c, z],
+            chip(other),
+        )
+
+    def spread(c, other, peer, source):
+        return remote(
+            source, xbufs[c].at[bucket, other],
+            m_send.at[c, peer, other], m_recv.at[c, bucket, other], (peer, seq),
+        )
+
+    def columns_of(which):
+        return pl.ds(pl.multiple_of(which * cols, 128), cols)
+
+    def result(c, peer, which):
+        place = out_ref.at[pl.ds(*chunks[c]), columns_of(which)]
+        return remote(
+            ybufs[c].at[peer], place, y_send.at[c, peer], y_recv.at[c, which], (peer, seq)
+        )
+
+    @pl.when(alive)
+    def _():
+        for other in others:
+            send_keys(0, other).start()
+        for other in others:
+            send_queries(0, other).start()
+        for other in others:
+            send_keys(1, other).start()
+        for c in range(1, count):
+            for other in others:
+                send_queries(c, other).start()
+        share(0, z, core).start()
+        share(1, z, core).start()
+
+    for c, (start, size) in enumerate(chunks):
+        qbufs[c][z] = own[0, start:start + size, mine]
+
+    def take_keys(kind):
+        for other in others:
+            @pl.when(holds(other, core))
+            def _():
+                place = kvbuf.at[kind, other * CORES + core]
+                remote(
+                    place, place, a_send.at[kind, other], a_recv.at[kind, other], partner
+                ).wait_recv()
+                share(kind, other, core).start()
+
+    def take_shared(kind):
+        for other in range(nz):
+            @pl.when(holds(other, 1 - core))
+            def _():
+                share(kind, other, 1 - core).wait_recv()
+
+    def take_queries(c):
+        for other in others:
+            @pl.when(holds(other, core))
+            def _():
+                place = qbufs[c].at[other]
+                remote(
+                    place, place, q_send.at[c, other], q_recv.at[c, other], partner
+                ).wait_recv()
+
+    length = len_ref[0]
+    heads = [slice(h * HEAD_DIM, (h + 1) * HEAD_DIM) for h in range(span // HEAD_DIM)]
+
+    def weigh(c, key_all):
+        size = chunks[c][1]
+        query_all = stack_rows([qbufs[c][i] for i in range(nz)])
+        usable = lax.broadcasted_iota(jnp.int32, (last * rows, nz * size), 0) < length
+        probs = []
+        for lanes in heads:
+            scores = lax.dot_general(
+                key_all[:, lanes], query_all[:, lanes], (((1,), (1,)), ((), ())),
+                preferred_element_type=jnp.float32,
+            ) * HEAD_DIM ** (-0.5)
+            scores = jnp.where(usable, scores, NEG_FILL)
+            top = jnp.max(scores, axis=0, keepdims=True)
+            prob = jnp.exp(scores - top)
+            probs.append((prob.astype(jnp.bfloat16), jnp.sum(prob, axis=0, keepdims=True)))
+        return probs
+
+    def attend(c, probs, value_all):
+        start, size = chunks[c]
+        lane = lax.broadcasted_iota(jnp.int32, (1, nz * size), 1)
+        block = lane // size
+        token = (block * CORES + core) * rows + start + (lane - block * size)
+        for lanes, (prob, total) in zip(heads, probs):
+            summed = lax.dot_general(
+                value_all[:, lanes], prob, (((0,), (0,)), ((), ())),
+                preferred_element_type=jnp.float32,
+            )
+            normal = jnp.where(token < length, summed / total, 0.0).T
+            for i in range(nz):
+                atts[c][i, :, lanes] = normal[i * size:(i + 1) * size].astype(jnp.bfloat16)
+        for other in others:
+            @pl.when(holds(other, core))
+            def _():
+                back(c, other).start()
+
+    take_keys(0)
+    take_queries(0)
+    take_shared(0)
+    key_all = stack_rows([kvbuf[0, j] for j in range(last)])
+    probs = weigh(0, key_all)
+    take_keys(1)
+    take_shared(1)
+    value_all = stack_rows([kvbuf[1, j] for j in range(last)])
+    attend(0, probs, value_all)
+    for c in range(1, count):
+        take_queries(c)
+        attend(c, weigh(c, key_all), value_all)
+
+    @pl.when(alive)
+    def _():
+        for c in range(count):
+            for peer in reversed(peers):
+                spread(c, z, peer, atts[c].at[z]).start()
+            xbufs[c][bucket, z] = atts[c][z]
+            for other in others:
+                place = xbufs[c].at[bucket, other]
+                remote(place, place, r_send.at[c, other], r_recv.at[c, other], partner).wait_recv()
+                for peer in reversed(peers):
+                    spread(c, other, peer, place).start()
+
+    w_copy.wait()
+
+    @pl.when(alive)
+    def _():
+        for c, (start, size) in enumerate(chunks):
+            for which in [bucket] + peers:
+                if which is not bucket:
+                    for other in range(nz):
+                        place = xbufs[c].at[which, other]
+                        remote(
+                            place, place, m_send.at[c, which, other], m_recv.at[c, which, other],
+                            partner,
+                        ).wait_recv()
+                left = jnp.concatenate([xbufs[c][which, i] for i in range(nz)], axis=1)
+                value = jnp.dot(
+                    left, weight[...], preferred_element_type=jnp.float32
+                ).astype(jnp.bfloat16)
+                if which is bucket:
+                    out_ref[start:start + size, columns_of(bucket)] = value
+                else:
+                    ybufs[c][which] = value
+                    result(c, which, bucket).start()
+        for c in range(count):
+            for peer in peers:
+                result(c, peer, peer).wait_recv()
+        for c in range(count):
+            for peer in peers:
+                result(c, peer, bucket).wait_send()
+                spread(c, z, peer, atts[c].at[z]).wait_send()
+                for other in others:
+                    spread(c, other, peer, xbufs[c].at[bucket, other]).wait_send()
+            for other in others:
+                send_queries(c, other).wait_send()
+        for kind in range(2):
+            for other in others:
+                send_keys(kind, other).wait_send()
+
+    for other in others:
+        @pl.when(holds(other, core))
+        def _():
+            for c in range(count):
+                back(c, other).wait_send()
+    for other in range(nz):
+        @pl.when(holds(other, core))
+        def _():
+            for kind in range(2):
+                share(kind, other, core).wait_send()
+
+
+def fused_shards(nb, nz, queries, keys, values, bucket_lens, gate, out_weight):
+    rows, width = queries.shape[1:]
+    cols = out_weight.shape[1]
+    span = width // nz
+    chunks = row_chunks(rows)
+    count = len(chunks)
+    low = jnp.bfloat16
+    dma = pltpu.SemaphoreType.DMA
+    anywhere = pl.BlockSpec(memory_space=pl.ANY)
+    projected = pl.pallas_call(
+        functools.partial(fused_kernel, nb, nz, chunks),
+        out_shape=pltpu.VMEM((rows, nb * cols), low),
+        in_specs=[pl.BlockSpec(memory_space=pltpu.SMEM)] + [anywhere] * 4,
+        out_specs=pl.BlockSpec(memory_space=pltpu.VMEM),
+        scratch_shapes=[
+            pltpu.VMEM((3, rows, width), low),
+            pltpu.VMEM((width, cols), low),
+            pltpu.VMEM((2, nz * CORES, rows, span), low),
+            dma((3,)), dma((2,)), dma,
+            dma((2, nz)), dma((2, nz)),
+            dma((count, nz)), dma((count, nz)),
+            dma((2, nz)), dma((2, nz)),
+            dma((count, nz)), dma((count, nz)),
+            dma((count, nb, nz)), dma((count, nb, nz)),
+            dma((count, nb)), dma((count, nb)),
+        ]
+        + [pltpu.VMEM((nz, size, span), low) for _, size in chunks]
+        + [pltpu.VMEM((nz, size, span), low) for _, size in chunks]
+        + [pltpu.VMEM((nb, nz, size, span), low) for _, size in chunks]
+        + [pltpu.VMEM((nb, size, cols), low) for _, size in chunks],
+        compiler_params=pltpu.CompilerParams(collective_id=0, has_side_effects=True),
+    )(bucket_lens, queries, keys, values, out_weight)
+    position = lax.axis_index("seq") * rows + lax.iota(jnp.int32, rows)
+    gated = projected.astype(jnp.float32) * gate[0][None, :]
+    keep = (position < bucket_lens[0])[:, None]
+    return jnp.where(keep, gated, 0.0).astype(jnp.bfloat16)[None]
+
+
 def solution(mesh):
     placed = (
         P("bucket", "seq", None),
@@ -80,6 +389,10 @@
         P("bucket", None),
         P(None, "bucket"),
     )
+    nb, ns = mesh.shape["bucket"], mesh.shape["seq"]
+    body = shards
+    if ns % CORES == 0 and HEADS % (ns // CORES) == 0:
+        body = functools.partial(fused_shards, nb, ns // CORES)
     return jax.shard_map(
-        shards, mesh=mesh, in_specs=placed, out_specs=P("bucket", "seq", None), check_vma=False
-    )
+        body, mesh=mesh, in_specs=placed, out_specs=P("bucket", "seq", None), check_vma=False
+    )

time: 150 us -> 38.1 us (0.25)
  waiting for transfers between devices: 62.4 us -> 0 us
  local copies, waits for them, and re-layouts: 36.7 us -> 0.01 us
  Pallas kernels: 0 us -> 36.4 us
  other arithmetic: 14.5 us -> 0.85 us
  between operations: 14.3 us -> 0.69 us
  starting transfers between devices: 11.7 us -> 0 us
  matrix products: 9.18 us -> 0 us
    pallas_call x0 -> x1, Pallas kernels: none -> 36.4 us  [fused_shards(): pl.pallas_call(functools.partial(fused_kernel, nb, nz, chunks), out_shape...]
    all_to_all x3 -> x0, waiting for transfers between devices: 34.3 us -> none  [the longest x1 30.8 us: shards(): lax.all_to_all(partial_value.reshape(1, count_all, width), 'seq', split_a...]
    all_gather x2 -> x0, waiting for transfers between devices: 26.6 us -> none  [the longest x1 26.6 us: shards(): queries_all = lax.all_gather(queries[0], 'seq', axis=0, tiled=True)]
    unnamed x15 -> x2, local copies, waits for them, and re-layouts: 12.6 us -> 0.01 us
    unnamed x3 -> x0, other arithmetic: 12.5 us -> none
    all_to_all x3 -> x0, starting transfers between devices: 11.7 us -> none  [the longest x1 4.82 us: shards(): lax.all_to_all(partial_value.reshape(1, count_all, width), 'seq', split_a...]
    reshape x2 -> x0, local copies, waits for them, and re-layouts: 10.6 us -> none  [the longest x1 7.59 us: shards(): partial_value.reshape(1, count_all, width)]
    all_to_all x3 -> x0, local copies, waits for them, and re-layouts: 9.49 us -> none  [the longest x1 9.25 us: shards(): lax.all_to_all(partial_value.reshape(1, count_all, width), 'seq', split_a...]
  transfers between devices with their start and end apart: 5 -> 0, of which waited for: 3 -> 0; matrix products, arithmetic and copies ran while one was open for 36% -> 0% of each run, Pallas kernels for 0% -> 0%
where the time goes in v2:
time: 38.1 us; the launch traced here: 37.9 us
  Pallas kernels  36.4 us (96%)
  other arithmetic  0.85 us (2%)
  between operations  0.69 us (2%)
    pallas_call x1, Pallas kernels, fused_shards(): pl.pallas_call(functools.partial(fused_kernel, nb, nz, chunks), out_shape...  36.4 us
    broadcast_in_dim x1, other arithmetic, fused_shards(): return jnp.where(keep, gated, 0.0).astype(jnp.bfloat16)[None]  0.84 us

profile of v2, /device:TPU:0, one launch (start us, length us, event | category | flops | bytes accessed | tf_op | source)
XLA Modules:
  0.0 37.9 jit_solution(2793543213917156693)
XLA Ops:
  0.0 0.0 copy-start
  0.7 36.4 %shard_map.64 = bf16[56,3072]{1,0:T(8,128)(2,1)S(1)} custom-call(s32[1]{0:T(128)} %copy.7.len_ref, bf16[1,56,1536]{2,1,0:T(8,128)(2,1)} %q_hbm.1, bf16[1,56,1536]{2,1,0:T(8,128)(2,1)} %k_hbm.1, bf16[1,56,1536]{2,1,0:T(8,128)(2,1)} %v_hbm.1, bf16[1536,768]{1,0:T(8,128)(2,1)} %w_hbm.1), custom_call_target="tpu_custom_call" | custom-call | tf_op jit(solution)/shard_map/pallas_call | solution.py:354
  37.1 0.0 copy-done
  37.1 0.8 %fusion = bf16[1,56,3072]{2,1,0:T(8,128)(2,1)} fusion(bf16[56,3072]{1,0:T(8,128)(2,1)S(1)} %shard_map.64, f32[3072]{0:T(1024)S(1)} %bitcast.5, pred[56]{0:T(512)(128)(4,1)S(1)} %add_compare_fusion), kind=kLoop, calls=%fused_computation.1 | loop fusion | flops 688128 | bytes 700472 | tf_op jit(solution)/shard_map/broadcast_in_dim | solution.py:380
  (1 shorter events, 0.0 us)
Async XLA Ops:
  0.0 37.1 %copy-start = (f32[1,3072]{1,0:T(1,128)S(1)}, f32[1,3072]{1,0:T(1,128)}, u32[]{:S(2)}) copy-start(f32[1,3072]{1,0:T(1,128)} %param.10) | copy-start | bytes 36868

commit v3 on v2

--- a/solution.py
+++ b/solution.py
@@ -110,7 +110,7 @@
     core = lax.rem(seq, CORES)
     last = nz * CORES - 1
     alive = seq < last
-    steps = [1, nz - 1] + list(range(2, nz - 1)) if nz > 2 else list(range(1, nz))
+    steps = list(range(2, nz - 1)) + [1, nz - 1] if nz > 2 else list(range(1, nz))
     others = [lax.rem(z + step, nz) for step in steps]
     peers = [lax.rem(bucket + step, nb) for step in range(1, nb)]
     if nb & (nb - 1) == 0:
@@ -268,6 +268,12 @@
             def _():
                 back(c, other).start()
 
+        @pl.when(alive)
+        def _():
+            for peer in peers:
+                spread(c, z, peer, atts[c].at[z]).start()
+            xbufs[c][bucket, z] = atts[c][z]
+
     take_keys(0)
     take_queries(0)
     take_shared(0)
@@ -284,13 +290,10 @@
     @pl.when(alive)
     def _():
         for c in range(count):
-            for peer in reversed(peers):
-                spread(c, z, peer, atts[c].at[z]).start()
-            xbufs[c][bucket, z] = atts[c][z]
             for other in others:
                 place = xbufs[c].at[bucket, other]
                 remote(place, place, r_send.at[c, other], r_recv.at[c, other], partner).wait_recv()
-                for peer in reversed(peers):
+                for peer in peers:
                     spread(c, other, peer, place).start()
 
     w_copy.wait()

time: 38.1 us -> 36.6 us (0.961)
  Pallas kernels: 36.4 us -> 34.6 us
    pallas_call x1, Pallas kernels: 36.4 us -> 34.6 us  [fused_shards(): pl.pallas_call(functools.partial(fused_kernel, nb, nz, chunks), out_shape...]
where the time goes in v3:
time: 36.6 us; the launch traced here: 36.1 us
  Pallas kernels  34.6 us (95%)
  other arithmetic  0.85 us (2%)
  between operations  0.69 us (2%)
    pallas_call x1, Pallas kernels, fused_shards(): pl.pallas_call(functools.partial(fused_kernel, nb, nz, chunks), out_shape...  34.6 us
    broadcast_in_dim x1, other arithmetic, fused_shards(): return jnp.where(keep, gated, 0.0).astype(jnp.bfloat16)[None]  0.84 us

profile of v3, /device:TPU:0, one launch (start us, length us, event | category | flops | bytes accessed | tf_op | source)
XLA Modules:
  0.0 36.1 jit_solution(1630777206923941490)
XLA Ops:
  0.0 0.0 copy-start
  0.7 34.6 %shard_map.64 = bf16[56,3072]{1,0:T(8,128)(2,1)S(1)} custom-call(s32[1]{0:T(128)} %copy.7.len_ref, bf16[1,56,1536]{2,1,0:T(8,128)(2,1)} %q_hbm.1, bf16[1,56,1536]{2,1,0:T(8,128)(2,1)} %k_hbm.1, bf16[1,56,1536]{2,1,0:T(8,128)(2,1)} %v_hbm.1, bf16[1536,768]{1,0:T(8,128)(2,1)} %w_hbm.1), custom_call_target="tpu_custom_call" | custom-call | tf_op jit(solution)/shard_map/pallas_call | solution.py:357
  35.3 0.0 copy-done
  35.3 0.8 %fusion = bf16[1,56,3072]{2,1,0:T(8,128)(2,1)} fusion(bf16[56,3072]{1,0:T(8,128)(2,1)S(1)} %shard_map.64, f32[3072]{0:T(1024)S(1)} %bitcast.5, pred[56]{0:T(512)(128)(4,1)S(1)} %add_compare_fusion), kind=kLoop, calls=%fused_computation.1 | loop fusion | flops 688128 | bytes 700472 | tf_op jit(solution)/shard_map/broadcast_in_dim | solution.py:383
  (1 shorter events, 0.0 us)
Async XLA Ops:
  0.0 35.3 %copy-start = (f32[1,3072]{1,0:T(1,128)S(1)}, f32[1,3072]{1,0:T(1,128)}, u32[]{:S(2)}) copy-start(f32[1,3072]{1,0:T(1,128)} %param.10) | copy-start | bytes 36868
